TPU v7x, 128 devices: a whole 4x4x4 slice. The times are simulated.
128 devices in a mesh: lat: 16 (over z_hi, x, core), lon: 8 (over z_lo, y).
Axes of the slice: x: 4, y: 4, z: 4 (z_hi: 2, z_lo: 2; z = z_hi * 2 + z_lo), core: 2. Of those that a mesh axis runs over, the one named last changes fastest.
Arguments:
- ocean_state: bfloat16 [1, 192, 640, 768], P(None, 'lat', None, 'lon'), may hold values from -6 to 6
- zonal_kernel: bfloat16 [2, 5, 256, 640], replicated, may hold values from -0.15625 to 0.15625
- norm_gain: bfloat16 [2, 640], replicated, may hold values from 0.099609375 to 1.8984375
- input_weight: bfloat16 [2, 640, 1280], replicated, may hold values from -0.25 to 0.25
- output_weight: bfloat16 [2, 1280, 640], replicated, may hold values from -0.15625 to 0.15625
Outputs:
- state_out: bfloat16 [1, 192, 640, 768], P(None, 'lat', None, 'lon')
All inputs are finite; a program needn't handle non-finite values.
Results may differ from a plain program's by a relative error of at most 0.009.
Values may be sent and summed in bfloat16 or wider, within the bound.
A program may use at most 128 MiB of HBM per device.

v0:
```python
import functools

import numpy as np
import jax
import jax.numpy as jnp
from jax import lax
from jax.experimental import pallas as pl
from jax.experimental.pallas import tpu as pltpu
from jax.sharding import PartitionSpec as P

C = 640
FF = 1280
W = 768
TAPS = 256
KROWS = 5
BLOCKS = 2
LON = 8
ROWS = 12
SHARE = C // LON
COLS = W // LON
HALF = W // 2
GROUPS = 3
TILES = 9
MESH = pl.DeviceIdType.MESH
F32 = jnp.float32
BF16 = jnp.bfloat16


def unit_place(unit):
    device, third = divmod(unit, 3)
    half, quarter = divmod(device, 4)
    return ((2 * third + half) * 4 + quarter) * 32


def basis():
    w = np.arange(W)[:, None]
    f = np.arange(HALF)[None, :]
    angle = 2.0 * np.pi / W * ((w * f) % W)
    sine = np.where(f == 0, 1.0 - 2.0 * (w % 2), np.sin(angle))
    full = np.concatenate([np.cos(angle), sine], axis=1)
    placed = np.zeros_like(full)
    for unit in range(W // 32):
        at = unit_place(unit)
        placed[at : at + 32] = full[32 * unit : 32 * unit + 32]
    return placed


def row_weights(total):
    h = np.arange(total)
    quad = np.sin(np.pi * (h + 0.5) / total)
    return np.concatenate([np.zeros(2), quad, np.zeros(2)]).astype(np.float32)


def nt(a, b):
    return lax.dot_general(a, b, (((1,), (1,)), ((), ())), preferred_element_type=F32)


def nn(a, b):
    return lax.dot_general(a, b, (((1,), (0,)), ((), ())), preferred_element_type=F32)


def gelu(x):
    return 0.5 * x * (1.0 + lax.erf(x * 0.7071067811865476))


def swap4(tiles):
    v0, v1, v2, v3 = [t.astype(F32) for t in tiles]
    lane = lax.broadcasted_iota(jnp.int32, v0.shape, 1)
    low = lane < 64
    even = (lane & 32) == 0
    roll = lambda v, s: pltpu.roll(v, s, 1)
    u0 = jnp.where(low, v0, roll(v2, 64))
    u2 = jnp.where(low, roll(v0, 64), v2)
    u1 = jnp.where(low, v1, roll(v3, 64))
    u3 = jnp.where(low, roll(v1, 64), v3)
    outs = (
        jnp.where(even, u0, roll(u1, 32)),
        jnp.where(even, roll(u0, 96), u1),
        jnp.where(even, u2, roll(u3, 32)),
        jnp.where(even, roll(u2, 96), u3),
    )
    return [o.astype(BF16) for o in outs]


def loop(count, body):
    def step(i, carry):
        body(i)
        return carry

    lax.fori_loop(0, count, step, 0)


def kernel(
    quad_ref, gain_ref, x_hbm, kern_hbm, w1_hbm, w2_hbm, f_hbm, out_hbm,
    rows_in, xpos, r1, xr, spec, kf, yb, s2, r2, w1t, w2t, hid, nrm, gainb,
    fb, kraw, w1, w2,
    in_sem, load_sem, out_sem, a_send, a_recv, b_send, b_recv, h_send, h_recv,
):
    me = lax.axis_index("lon")
    lat = lax.axis_index("lat")
    lats = lax.axis_size("lat")
    up = lax.rem(lat + lats - 1, lats)
    down = lax.rem(lat + 1, lats)
    mine = pl.ds(pl.multiple_of(me * SHARE, SHARE), SHARE)

    def tiles_of(g):
        return pl.ds(3 * g, 3)

    def fetch(g):
        return pltpu.make_async_copy(
            x_hbm.at[0, pl.ds(4 * g, 4)], rows_in.at[pl.ds(4 * g, 4)], in_sem.at[g]
        )

    for g in range(GROUPS):
        fetch(g).start()
    loads = [
        pltpu.make_async_copy(src, dst, load_sem.at[i])
        for i, (src, dst) in enumerate(
            [(kern_hbm, kraw), (f_hbm, fb), (w1_hbm, w1), (w2_hbm, w2)]
        )
    ]
    for copy in loads:
        copy.start()

    barrier = pltpu.get_barrier_semaphore()
    for d in range(1, LON):
        pl.semaphore_signal(
            barrier, inc=1, device_id={"lon": lax.rem(me + d, LON)}, device_id_type=MESH
        )
    for other in (up, down):
        pl.semaphore_signal(barrier, inc=1, device_id={"lat": other}, device_id_type=MESH)

    def a_copy(l, g, d):
        peer = lax.rem(me + d, LON)
        theirs = pl.ds(pl.multiple_of(peer * SHARE, SHARE), SHARE)
        return pltpu.make_async_remote_copy(
            src_ref=xpos.at[l, tiles_of(g), theirs],
            dst_ref=r1.at[l, me, tiles_of(g)],
            send_sem=a_send.at[l, g, d - 1],
            recv_sem=a_recv.at[l, g, d - 1],
            device_id={"lon": peer},
            device_id_type=MESH,
        )

    def b_copy(l, g, d):
        peer = lax.rem(me + d, LON)
        return pltpu.make_async_remote_copy(
            src_ref=s2.at[l, peer, tiles_of(g)],
            dst_ref=r2.at[l, tiles_of(g), mine],
            send_sem=b_send.at[l, g, d - 1],
            recv_sem=b_recv.at[l, g, d - 1],
            device_id={"lon": peer},
            device_id_type=MESH,
        )

    def halo_copy(l, side):
        src, dst, other = ((2, 14, up), (12, 0, down))[side]
        return pltpu.make_async_remote_copy(
            src_ref=xr.at[l, pl.ds(src, 2)],
            dst_ref=xr.at[l, pl.ds(dst, 2)],
            send_sem=h_send.at[l, side],
            recv_sem=h_recv.at[l, side],
            device_id={"lat": other},
            device_id_type=MESH,
        )

    def start_a(l, g):
        for d in range(1, LON):
            a_copy(l, g, d).start()
        r1[l, me, tiles_of(g)] = xpos[l, tiles_of(g), mine]

    def pack_input(g):
        def piece(i):
            rows = pl.ds(pl.multiple_of(i * SHARE, SHARE), SHARE)
            pad = jnp.zeros((SHARE, 128 - COLS), BF16)
            tiles = [
                jnp.concatenate([rows_in[4 * g + r, rows, :], pad], axis=1) for r in range(4)
            ]
            packed = swap4(tiles)
            for third in range(3):
                xpos[0, 3 * g + third, rows, :] = packed[third]

        loop(C // SHARE, piece)

    for g in range(GROUPS):
        fetch(g).wait()
        pack_input(g)
        if g == 0:
            pl.semaphore_wait(barrier, LON + 1)
        start_a(0, g)

    loads[0].wait()
    loads[1].wait()
    taps_basis = [unit_place((32 * u - TAPS // 2) % W // 32) for u in range(TAPS // 32)]

    def spectra(i):
        l = i // KROWS
        r = lax.rem(i, KROWS)
        pick = (
            lax.broadcasted_iota(jnp.int32, (SHARE, C), 1)
            == lax.broadcasted_iota(jnp.int32, (SHARE, C), 0) + me * SHARE
        ).astype(BF16)
        taps = nt(pick, kraw[l, r]).astype(BF16)
        tap_rows = jnp.concatenate([fb[p : p + 32, :] for p in taps_basis], axis=0)
        full = nn(taps, tap_rows)
        keep = lax.broadcasted_iota(jnp.int32, (SHARE, HALF), 1) >= 1
        scale = jnp.where(keep, 2.0 / W, 1.0 / W).astype(F32)
        real = full[:, :HALF] * scale
        sine = full[:, HALF:] * scale
        kf[l, r, 0] = real
        kf[l, r, 1] = jnp.where(keep, sine, 0.0)
        kf[l, r, 2] = jnp.where(keep, real, sine)

    loop(BLOCKS * KROWS, spectra)
    loads[2].wait()
    loads[3].wait()

    def unit_matrix(n):
        return (
            lax.broadcasted_iota(jnp.int32, (n, n), 0)
            == lax.broadcasted_iota(jnp.int32, (n, n), 1)
        ).astype(BF16)

    for l in range(BLOCKS):

        def turn1(i):
            at = pl.ds(pl.multiple_of(i * 256, 256), 256)
            w1t[l, at, :] = nt(unit_matrix(256), w1[l, :, at]).astype(BF16)

        def turn2(i):
            at = pl.ds(pl.multiple_of(i * 128, 128), 128)
            w2t[l, at, :] = nt(unit_matrix(128), w2[l, :, at]).astype(BF16)
            row = jnp.broadcast_to(gain_ref[pl.ds(l, 1), at].astype(F32), (128, 128))
            gainb[l, at, :] = row.T

        loop(FF // 256, turn1)
        loop(C // 128, turn2)

    def unpack(l, g):
        def piece(third):
            for half in range(2):
                tiles = [r1[l, 4 * half + q, 3 * g + third] for q in range(4)]
                rows = swap4(tiles)
                at = pl.ds(pl.multiple_of(256 * third, 128) + 128 * half, 128)
                for r in range(4):
                    xr[l, 2 + 4 * g + r, :, at] = rows[r]

        loop(3, piece)

    def transform(l, first, count):
        def piece(n):
            at = pl.ds(pl.multiple_of(n * 256, 256), 256)
            lhs = xr[l, pl.ds(first, count)].reshape(count * SHARE, W)
            part = nn(lhs, fb[:, at])
            for r in range(count):
                weight = quad_ref[lat * ROWS + first + r]
                spec[first + r, :, at] = part[SHARE * r : SHARE * (r + 1)] * weight

        loop(3, piece)

    def convolve(l, g):
        def bands(i):
            rows = pl.ds(pl.multiple_of(i * 16, 16), 16)
            for n in range(3):
                re_at = pl.ds(128 * n, 128)
                im_at = pl.ds(HALF + 128 * n, 128)
                factors = [
                    [kf[l, r, j, rows, re_at] for j in range(3)] for r in range(KROWS)
                ]
                for row in range(4):
                    real = sine = None
                    for r in range(KROWS):
                        a = spec[4 * g + row + r, rows, re_at]
                        b = spec[4 * g + row + r, rows, im_at]
                        kr, kc, ks = factors[r]
                        new_real = a * kr - b * kc
                        new_sine = a * kc + b * ks
                        real = new_real if real is None else real + new_real
                        sine = new_sine if sine is None else sine + new_sine
                    yb[row, rows, re_at] = real.astype(BF16)
                    yb[row, rows, im_at] = sine.astype(BF16)

        loop(SHARE // 16, bands)

        def invert(third):
            at = pl.multiple_of(256 * third, 256)
            lhs = yb[...].reshape(4 * SHARE, W)
            part = nt(lhs, fb[pl.ds(at, 256), :])
            for half in range(2):
                tiles = []
                for r in range(4):
                    conv = part[SHARE * r : SHARE * (r + 1), 128 * half : 128 * (half + 1)]
                    old = xr[l, 2 + 4 * g + r, :, pl.ds(at + 128 * half, 128)]
                    tiles.append((old.astype(F32) + gelu(conv)).astype(BF16))
                packed = swap4(tiles)
                for q in range(4):
                    s2[l, 4 * half + q, 3 * g + third] = packed[q]

        loop(3, invert)

    def start_b(l, g):
        for d in range(1, LON):
            b_copy(l, g, d).start()
        r2[l, tiles_of(g), mine] = s2[l, me, tiles_of(g)]

    def feed_forward(l, g):
        def norm(t):
            values = r2[l, 3 * g + t].astype(F32)
            average = jnp.sum(values, axis=0, keepdims=True) * (1.0 / C)
            centred = values - average
            variance = jnp.sum(centred * centred, axis=0, keepdims=True) * (1.0 / C)
            scaled = centred * lax.rsqrt(variance + 1e-05) * gainb[l]
            nrm[:, pl.ds(pl.multiple_of(128 * t, 128), 128)] = scaled.astype(BF16)

        loop(3, norm)

        def first(i):
            at = pl.ds(pl.multiple_of(i * 256, 256), 256)
            hid[at, :] = gelu(nn(w1t[l, at, :], nrm[...])).astype(BF16)

        loop(FF // 256, first)

        def second(i):
            at = pl.ds(pl.multiple_of(i * 128, 128), 128)
            out = nn(w2t[l, at, :], hid[...])
            for t in range(3):
                old = r2[l, 3 * g + t, at, :].astype(F32)
                new = (old + out[:, 128 * t : 128 * (t + 1)]).astype(BF16)
                xpos[(l + 1) % 2, 3 * g + t, at, :] = new

        loop(C // 128, second)

    def finish(g):
        def piece(i):
            rows = pl.ds(pl.multiple_of(i * SHARE, SHARE), SHARE)
            tiles = [xpos[0, 3 * g + t, rows, :] for t in (0, 1, 2, 2)]
            apart = swap4(tiles)
            for r in range(4):
                rows_in[4 * g + r, rows, :] = apart[r][:, :COLS]

        loop(C // SHARE, piece)

    def store(g):
        return pltpu.make_async_copy(
            rows_in.at[pl.ds(4 * g, 4)], out_hbm.at[0, pl.ds(4 * g, 4)], out_sem.at[g]
        )

    order = (1, 0, 2)
    for l in range(BLOCKS):
        for g in (0, 1, 2) if l == 0 else order:
            for d in range(1, LON):
                a_copy(l, g, d).wait_recv()
            unpack(l, g)
            if g == 0:
                halo_copy(l, 0).start()
            if g == 2:
                halo_copy(l, 1).start()
            transform(l, 2 + 4 * g, 4)
        if l == 1:
            pass
        for g in order:
            if g == 0:
                halo_copy(l, 1).wait_recv()
                transform(l, 0, 2)
            if g == 2:
                halo_copy(l, 0).wait_recv()
                transform(l, 14, 2)
            convolve(l, g)
            start_b(l, g)
        if l == 1:
            pass
        if l == 0:
            pass
        for g in order:
            for d in range(1, LON):
                b_copy(l, g, d).wait_recv()
            if l == 1:
                for d in range(1, LON):
                    a_copy(0, g, d).wait_send()
            feed_forward(l, g)
            if l == 0:
                start_a(1, g)
            else:
                finish(g)
                store(g).start()
    for g in range(GROUPS):
        for d in range(1, LON):
            a_copy(1, g, d).wait_send()
            b_copy(0, g, d).wait_send()
            b_copy(1, g, d).wait_send()
        store(g).wait()
    for l in range(BLOCKS):
        for side in range(2):
            halo_copy(l, side).wait_send()


def body(ocean_state, zonal_kernel, norm_gain, input_weight, output_weight):
    total = ROWS * lax.axis_size("lat")
    quad = jnp.asarray(row_weights(total))
    table = jnp.asarray(basis().astype(jnp.bfloat16))
    hbm = pl.BlockSpec(memory_space=pl.ANY)
    return pl.pallas_call(
        kernel,
        out_shape=jax.ShapeDtypeStruct((1, ROWS, C, COLS), BF16),
        in_specs=[
            pl.BlockSpec(memory_space=pltpu.SMEM),
            pl.BlockSpec(memory_space=pltpu.VMEM),
            hbm, hbm, hbm, hbm, hbm,
        ],
        out_specs=hbm,
        scratch_shapes=[
            pltpu.VMEM((ROWS, C, COLS), BF16),
            pltpu.VMEM((2, TILES, C, 128), BF16),
            pltpu.VMEM((2, LON, TILES, SHARE, 128), BF16),
            pltpu.VMEM((2, ROWS + 4, SHARE, W), BF16),
            pltpu.VMEM((ROWS + 4, SHARE, W), F32),
            pltpu.VMEM((2, KROWS, 3, SHARE, HALF), F32),
            pltpu.VMEM((4, SHARE, W), BF16),
            pltpu.VMEM((2, LON, TILES, SHARE, 128), BF16),
            pltpu.VMEM((2, TILES, C, 128), BF16),
            pltpu.VMEM((2, FF, C), BF16),
            pltpu.VMEM((2, C, FF), BF16),
            pltpu.VMEM((FF, 384), BF16),
            pltpu.VMEM((C, 384), BF16),
            pltpu.VMEM((2, C, 128), F32),
            pltpu.VMEM((W, W), BF16),
            pltpu.VMEM((BLOCKS, KROWS, TAPS, C), BF16),
            pltpu.VMEM((BLOCKS, C, FF), BF16),
            pltpu.VMEM((BLOCKS, FF, C), BF16),
            pltpu.SemaphoreType.DMA((GROUPS,)),
            pltpu.SemaphoreType.DMA((4,)),
            pltpu.SemaphoreType.DMA((GROUPS,)),
            pltpu.SemaphoreType.DMA((2, GROUPS, LON - 1)),
            pltpu.SemaphoreType.DMA((2, GROUPS, LON - 1)),
            pltpu.SemaphoreType.DMA((2, GROUPS, LON - 1)),
            pltpu.SemaphoreType.DMA((2, GROUPS, LON - 1)),
            pltpu.SemaphoreType.DMA((2, 2)),
            pltpu.SemaphoreType.DMA((2, 2)),
        ],
        compiler_params=pltpu.CompilerParams(
            collective_id=0, has_side_effects=True, vmem_limit_bytes=62 * 1024 * 1024
        ),
    )(quad, norm_gain, ocean_state, zonal_kernel, input_weight, output_weight, table)


def solution(mesh):
    in_specs = (P(None, "lat", None, "lon"), P(), P(), P(), P())
    out_specs = P(None, "lat", None, "lon")
    return jax.shard_map(body, mesh=mesh, in_specs=in_specs, out_specs=out_specs, check_vma=False)
```

profile of v0, /device:TPU:64, one launch (start us, length us, event | category | flops | bytes accessed | tf_op | source)
XLA Modules:
  0.0 107.0 jit_solution(771380952331841862)
XLA Ops:
  0.0 3.7 %copy.8.x_hbm = bf16[1,12,640,96]{3,2,1,0:T(8,128)(2,1)} copy(bf16[1,12,640,96]{2,3,1,0:T(8,128)(2,1)} %param.7) | data formatting | bytes 2949120 | tf_op args[0]
  3.7 99.4 %shard_map.73 = bf16[1,12,640,96]{3,2,1,0:T(8,128)(2,1)} custom-call(f32[196]{0:T(256)} %constant.4.clone.quad_ref, bf16[2,640]{1,0:T(2,128)(2,1)} %gain_ref.1, bf16[1,12,640,96]{3,2,1,0:T(8,128)(2,1)} %copy.8.x_hbm, bf16[2,5,256,640]{3,2,1,0:T(8,128)(2,1)} %kern_hbm.1, bf16[2,640,1280]{2,1,0:T(8,128)(2,1)} %w1_hbm.1, bf16[2,1280,640]{2,1,0:T(8,128)(2,1)} %w2_hbm.1, ...), custom_call_target="tpu_custom_call" | custom-call | tf_op jit(solution)/shard_map/pallas_call | solution.py:402
  103.2 3.8 %copy.9 = bf16[1,12,640,96]{2,3,1,0:T(8,128)(2,1)} copy(bf16[1,12,640,96]{3,2,1,0:T(8,128)(2,1)} %shard_map.73) | data formatting | bytes 2949120 | tf_op jit(solution)/shard_map/pallas_call | solution.py:402
where the time goes:
time: 107 us
  Pallas kernels  99.4 us (93%)
  local copies, waits for them, and re-layouts  7.53 us (7%)
    pallas_call x1, Pallas kernels, body(): pl.pallas_call(kernel, out_shape=jax.ShapeDtypeStruct((1, ROWS, C, COLS),...  99.4 us
    pallas_call x1, local copies, waits for them, and re-layouts, body(): pl.pallas_call(kernel, out_shape=jax.ShapeDtypeStruct((1, ROWS, C, COLS),...  3.78 us
    unnamed x1, local copies, waits for them, and re-layouts  3.75 us

commit v1 on v0

--- a/solution.py
+++ b/solution.py
@@ -20,6 +20,9 @@
 COLS = W // LON
 HALF = W // 2
 GROUPS = 3
+SPLIT = 32
+A_ORDER = ((0, 1, 2), (1, 2, 0))
+B_ORDER = ((1, 2, 0), (1, 0, 2))
 TILES = 9
 MESH = pl.DeviceIdType.MESH
 F32 = jnp.float32
@@ -64,7 +67,7 @@
 
 
 def swap4(tiles):
-    v0, v1, v2, v3 = [t.astype(F32) for t in tiles]
+    v0, v1, v2, v3 = tiles
     lane = lax.broadcasted_iota(jnp.int32, v0.shape, 1)
     low = lane < 64
     even = (lane & 32) == 0
@@ -73,13 +76,12 @@
     u2 = jnp.where(low, roll(v0, 64), v2)
     u1 = jnp.where(low, v1, roll(v3, 64))
     u3 = jnp.where(low, roll(v1, 64), v3)
-    outs = (
+    return (
         jnp.where(even, u0, roll(u1, 32)),
         jnp.where(even, roll(u0, 96), u1),
         jnp.where(even, u2, roll(u3, 32)),
         jnp.where(even, roll(u2, 96), u3),
     )
-    return [o.astype(BF16) for o in outs]
 
 
 def loop(count, body):
@@ -93,7 +95,7 @@
 def kernel(
     quad_ref, gain_ref, x_hbm, kern_hbm, w1_hbm, w2_hbm, f_hbm, out_hbm,
     rows_in, xpos, r1, xr, spec, kf, yb, s2, r2, w1t, w2t, hid, nrm, gainb,
-    fb, kraw, w1, w2,
+    fb, fbt, kraw, w1, w2,
     in_sem, load_sem, out_sem, a_send, a_recv, b_send, b_recv, h_send, h_recv,
 ):
     me = lax.axis_index("lon")
@@ -130,25 +132,39 @@
     for other in (up, down):
         pl.semaphore_signal(barrier, inc=1, device_id={"lat": other}, device_id_type=MESH)
 
-    def a_copy(l, g, d):
+    def a_parts(l, g):
+        if g == A_ORDER[l][2]:
+            return [(2, 0, SPLIT), (3, SPLIT, SHARE - SPLIT)]
+        return [(A_ORDER[l].index(g), 0, SHARE)]
+
+    def b_parts(l, g):
+        if g == B_ORDER[l][0]:
+            return [(0, 0, SPLIT), (1, SPLIT, SHARE - SPLIT)]
+        return [(1 + B_ORDER[l].index(g), 0, SHARE)]
+
+    def channels(owner, first, count):
+        return pl.ds(pl.multiple_of(owner * SHARE + first, 16), count)
+
+    def a_copy(l, g, part, d):
+        slot, first, count = part
         peer = lax.rem(me + d, LON)
-        theirs = pl.ds(pl.multiple_of(peer * SHARE, SHARE), SHARE)
         return pltpu.make_async_remote_copy(
-            src_ref=xpos.at[l, tiles_of(g), theirs],
-            dst_ref=r1.at[l, me, tiles_of(g)],
-            send_sem=a_send.at[l, g, d - 1],
-            recv_sem=a_recv.at[l, g, d - 1],
+            src_ref=xpos.at[l, tiles_of(g), channels(peer, first, count)],
+            dst_ref=r1.at[l, me, tiles_of(g), pl.ds(first, count)],
+            send_sem=a_send.at[l, slot, d - 1],
+            recv_sem=a_recv.at[l, slot, d - 1],
             device_id={"lon": peer},
             device_id_type=MESH,
         )
 
-    def b_copy(l, g, d):
+    def b_copy(l, g, part, d):
+        slot, first, count = part
         peer = lax.rem(me + d, LON)
         return pltpu.make_async_remote_copy(
-            src_ref=s2.at[l, peer, tiles_of(g)],
-            dst_ref=r2.at[l, tiles_of(g), mine],
-            send_sem=b_send.at[l, g, d - 1],
-            recv_sem=b_recv.at[l, g, d - 1],
+            src_ref=s2.at[l, peer, tiles_of(g), pl.ds(first, count)],
+            dst_ref=r2.at[l, tiles_of(g), channels(me, first, count)],
+            send_sem=b_send.at[l, slot, d - 1],
+            recv_sem=b_recv.at[l, slot, d - 1],
             device_id={"lon": peer},
             device_id_type=MESH,
         )
@@ -165,22 +181,20 @@
         )
 
     def start_a(l, g):
-        for d in range(1, LON):
-            a_copy(l, g, d).start()
+        for part in a_parts(l, g):
+            for d in range(1, LON):
+                a_copy(l, g, part, d).start()
         r1[l, me, tiles_of(g)] = xpos[l, tiles_of(g), mine]
 
     def pack_input(g):
         def piece(i):
-            rows = pl.ds(pl.multiple_of(i * SHARE, SHARE), SHARE)
-            pad = jnp.zeros((SHARE, 128 - COLS), BF16)
-            tiles = [
-                jnp.concatenate([rows_in[4 * g + r, rows, :], pad], axis=1) for r in range(4)
-            ]
-            packed = swap4(tiles)
+            at = pl.ds(pl.multiple_of(i * 128, 128), 128)
             for third in range(3):
-                xpos[0, 3 * g + third, rows, :] = packed[third]
-
-        loop(C // SHARE, piece)
+                lons = pl.ds(32 * third, 32)
+                tile = jnp.concatenate([rows_in[4 * g + r, lons, at] for r in range(4)], axis=0)
+                xpos[0, 3 * g + third, at, :] = tile.T
+
+        loop(C // 128, piece)
 
     for g in range(GROUPS):
         fetch(g).wait()
@@ -188,6 +202,12 @@
         if g == 0:
             pl.semaphore_wait(barrier, LON + 1)
         start_a(0, g)
+
+    def unit_matrix(n):
+        return (
+            lax.broadcasted_iota(jnp.int32, (n, n), 0)
+            == lax.broadcasted_iota(jnp.int32, (n, n), 1)
+        ).astype(BF16)
 
     loads[0].wait()
     loads[1].wait()
@@ -212,14 +232,14 @@
         kf[l, r, 2] = jnp.where(keep, real, sine)
 
     loop(BLOCKS * KROWS, spectra)
+
+    def turn0(i):
+        at = pl.ds(pl.multiple_of(i * 256, 256), 256)
+        fbt[at, :] = nt(unit_matrix(256), fb[:, at]).astype(BF16)
+
+    loop(W // 256, turn0)
     loads[2].wait()
     loads[3].wait()
-
-    def unit_matrix(n):
-        return (
-            lax.broadcasted_iota(jnp.int32, (n, n), 0)
-            == lax.broadcasted_iota(jnp.int32, (n, n), 1)
-        ).astype(BF16)
 
     for l in range(BLOCKS):
 
@@ -236,31 +256,37 @@
         loop(FF // 256, turn1)
         loop(C // 128, turn2)
 
-    def unpack(l, g):
+    def unpack(l, g, first, count):
+        some = pl.ds(first, count)
+
         def piece(third):
             for half in range(2):
-                tiles = [r1[l, 4 * half + q, 3 * g + third] for q in range(4)]
+                tiles = [r1[l, 4 * half + q, 3 * g + third, some, :] for q in range(4)]
                 rows = swap4(tiles)
                 at = pl.ds(pl.multiple_of(256 * third, 128) + 128 * half, 128)
                 for r in range(4):
-                    xr[l, 2 + 4 * g + r, :, at] = rows[r]
+                    xr[l, 2 + 4 * g + r, some, at] = rows[r]
 
         loop(3, piece)
 
-    def transform(l, first, count):
+    def transform(l, top, rows, first, count):
+        some = pl.ds(first, count)
+
         def piece(n):
             at = pl.ds(pl.multiple_of(n * 256, 256), 256)
-            lhs = xr[l, pl.ds(first, count)].reshape(count * SHARE, W)
+            lhs = xr[l, pl.ds(top, rows), some, :].reshape(rows * count, W)
             part = nn(lhs, fb[:, at])
-            for r in range(count):
-                weight = quad_ref[lat * ROWS + first + r]
-                spec[first + r, :, at] = part[SHARE * r : SHARE * (r + 1)] * weight
+            for r in range(rows):
+                weight = quad_ref[lat * ROWS + top + r]
+                spec[top + r, some, at] = part[count * r : count * (r + 1)] * weight
 
         loop(3, piece)
 
-    def convolve(l, g):
+    def convolve(l, g, first, count):
+        some = pl.ds(first, count)
+
         def bands(i):
-            rows = pl.ds(pl.multiple_of(i * 16, 16), 16)
+            rows = pl.ds(pl.multiple_of(first + i * 16, 16), 16)
             for n in range(3):
                 re_at = pl.ds(128 * n, 128)
                 im_at = pl.ds(HALF + 128 * n, 128)
@@ -280,28 +306,31 @@
                     yb[row, rows, re_at] = real.astype(BF16)
                     yb[row, rows, im_at] = sine.astype(BF16)
 
-        loop(SHARE // 16, bands)
+        loop(count // 16, bands)
 
         def invert(third):
             at = pl.multiple_of(256 * third, 256)
-            lhs = yb[...].reshape(4 * SHARE, W)
-            part = nt(lhs, fb[pl.ds(at, 256), :])
+            lhs = yb[:, some, :].reshape(4 * count, W)
+            part = nn(lhs, fbt[:, pl.ds(at, 256)])
             for half in range(2):
                 tiles = []
                 for r in range(4):
-                    conv = part[SHARE * r : SHARE * (r + 1), 128 * half : 128 * (half + 1)]
-                    old = xr[l, 2 + 4 * g + r, :, pl.ds(at + 128 * half, 128)]
+                    conv = part[count * r : count * (r + 1), 128 * half : 128 * (half + 1)]
+                    old = xr[l, 2 + 4 * g + r, some, pl.ds(at + 128 * half, 128)]
                     tiles.append((old.astype(F32) + gelu(conv)).astype(BF16))
                 packed = swap4(tiles)
                 for q in range(4):
-                    s2[l, 4 * half + q, 3 * g + third] = packed[q]
+                    s2[l, 4 * half + q, 3 * g + third, some, :] = packed[q]
 
         loop(3, invert)
 
-    def start_b(l, g):
+    def start_b(l, g, part):
+        slot, first, count = part
         for d in range(1, LON):
-            b_copy(l, g, d).start()
-        r2[l, tiles_of(g), mine] = s2[l, me, tiles_of(g)]
+            b_copy(l, g, part, d).start()
+        r2[l, tiles_of(g), channels(me, first, count)] = s2[
+            l, me, tiles_of(g), pl.ds(first, count)
+        ]
 
     def feed_forward(l, g):
         def norm(t):
@@ -315,93 +344,84 @@
         loop(3, norm)
 
         def first(i):
-            at = pl.ds(pl.multiple_of(i * 256, 256), 256)
+            at = pl.ds(pl.multiple_of(i * 640, 640), 640)
             hid[at, :] = gelu(nn(w1t[l, at, :], nrm[...])).astype(BF16)
 
-        loop(FF // 256, first)
-
-        def second(i):
-            at = pl.ds(pl.multiple_of(i * 128, 128), 128)
-            out = nn(w2t[l, at, :], hid[...])
-            for t in range(3):
-                old = r2[l, 3 * g + t, at, :].astype(F32)
-                new = (old + out[:, 128 * t : 128 * (t + 1)]).astype(BF16)
-                xpos[(l + 1) % 2, 3 * g + t, at, :] = new
-
-        loop(C // 128, second)
-
-    def finish(g):
-        def piece(i):
-            rows = pl.ds(pl.multiple_of(i * SHARE, SHARE), SHARE)
-            tiles = [xpos[0, 3 * g + t, rows, :] for t in (0, 1, 2, 2)]
-            apart = swap4(tiles)
-            for r in range(4):
-                rows_in[4 * g + r, rows, :] = apart[r][:, :COLS]
-
-        loop(C // SHARE, piece)
+        loop(FF // 640, first)
+        out = nn(w2t[l], hid[...])
+        for t in range(3):
+            old = r2[l, 3 * g + t].astype(F32)
+            new = (old + out[:, 128 * t : 128 * (t + 1)]).astype(BF16)
+            if l == 0:
+                xpos[1, 3 * g + t] = new
+            else:
+                lons = pl.ds(32 * t, 32)
+                for i in range(C // 128):
+                    turned = new[128 * i : 128 * (i + 1), :].T
+                    for r in range(4):
+                        rows_in[4 * g + r, lons, pl.ds(128 * i, 128)] = turned[
+                            32 * r : 32 * (r + 1), :
+                        ]
 
     def store(g):
         return pltpu.make_async_copy(
             rows_in.at[pl.ds(4 * g, 4)], out_hbm.at[0, pl.ds(4 * g, 4)], out_sem.at[g]
         )
 
-    order = (1, 0, 2)
+    def take(l, g, part):
+        for d in range(1, LON):
+            a_copy(l, g, part, d).wait_recv()
+        unpack(l, g, *part[1:])
+        if part[1] + part[2] == SHARE and g != 1:
+            halo_copy(l, g // 2).start()
+        transform(l, 2 + 4 * g, 4, *part[1:])
+
+    def give(l, g, part):
+        convolve(l, g, *part[1:])
+        start_b(l, g, part)
+
     for l in range(BLOCKS):
-        for g in (0, 1, 2) if l == 0 else order:
-            for d in range(1, LON):
-                a_copy(l, g, d).wait_recv()
-            unpack(l, g)
-            if g == 0:
-                halo_copy(l, 0).start()
-            if g == 2:
-                halo_copy(l, 1).start()
-            transform(l, 2 + 4 * g, 4)
-        if l == 1:
-            pass
-        for g in order:
-            if g == 0:
-                halo_copy(l, 1).wait_recv()
-                transform(l, 0, 2)
-            if g == 2:
-                halo_copy(l, 0).wait_recv()
-                transform(l, 14, 2)
-            convolve(l, g)
-            start_b(l, g)
-        if l == 1:
-            pass
-        if l == 0:
-            pass
-        for g in order:
-            for d in range(1, LON):
-                b_copy(l, g, d).wait_recv()
-            if l == 1:
+        for g in A_ORDER[l][:2]:
+            take(l, g, a_parts(l, g)[0])
+        last = A_ORDER[l][2]
+        for arrived, ready in zip(a_parts(l, last), b_parts(l, 1)):
+            take(l, last, arrived)
+            give(l, 1, ready)
+        for g in B_ORDER[l][1:]:
+            halo_copy(l, 1 - g // 2).wait_recv()
+            transform(l, 0 if g == 0 else ROWS + 2, 2, 0, SHARE)
+            give(l, g, b_parts(l, g)[0])
+        for g in B_ORDER[l]:
+            for part in b_parts(l, g):
                 for d in range(1, LON):
-                    a_copy(0, g, d).wait_send()
+                    b_copy(l, g, part, d).wait_recv()
             feed_forward(l, g)
             if l == 0:
                 start_a(1, g)
             else:
-                finish(g)
                 store(g).start()
-    for g in range(GROUPS):
-        for d in range(1, LON):
-            a_copy(1, g, d).wait_send()
-            b_copy(0, g, d).wait_send()
-            b_copy(1, g, d).wait_send()
-        store(g).wait()
     for l in range(BLOCKS):
+        for g in range(GROUPS):
+            for d in range(1, LON):
+                for part in a_parts(l, g):
+                    a_copy(l, g, part, d).wait_send()
+                for part in b_parts(l, g):
+                    b_copy(l, g, part, d).wait_send()
         for side in range(2):
             halo_copy(l, side).wait_send()
+    for g in range(GROUPS):
+        store(g).wait()
 
 
 def body(ocean_state, zonal_kernel, norm_gain, input_weight, output_weight):
     total = ROWS * lax.axis_size("lat")
     quad = jnp.asarray(row_weights(total))
     table = jnp.asarray(basis().astype(jnp.bfloat16))
+    state = jnp.transpose(ocean_state, (0, 1, 3, 2))
     hbm = pl.BlockSpec(memory_space=pl.ANY)
-    return pl.pallas_call(
+    out = pl.pallas_call(
         kernel,
-        out_shape=jax.ShapeDtypeStruct((1, ROWS, C, COLS), BF16),
+        out_shape=jax.ShapeDtypeStruct((1, ROWS, COLS, C), BF16),
         in_specs=[
             pl.BlockSpec(memory_space=pltpu.SMEM),
             pl.BlockSpec(memory_space=pltpu.VMEM),
@@ -409,7 +429,7 @@
         ],
         out_specs=hbm,
         scratch_shapes=[
-            pltpu.VMEM((ROWS, C, COLS), BF16),
+            pltpu.VMEM((ROWS, COLS, C), BF16),
             pltpu.VMEM((2, TILES, C, 128), BF16),
             pltpu.VMEM((2, LON, TILES, SHARE, 128), BF16),
             pltpu.VMEM((2, ROWS + 4, SHARE, W), BF16),
@@ -424,23 +444,25 @@
             pltpu.VMEM((C, 384), BF16),
             pltpu.VMEM((2, C, 128), F32),
             pltpu.VMEM((W, W), BF16),
+            pltpu.VMEM((W, W), BF16),
             pltpu.VMEM((BLOCKS, KROWS, TAPS, C), BF16),
             pltpu.VMEM((BLOCKS, C, FF), BF16),
             pltpu.VMEM((BLOCKS, FF, C), BF16),
             pltpu.SemaphoreType.DMA((GROUPS,)),
             pltpu.SemaphoreType.DMA((4,)),
             pltpu.SemaphoreType.DMA((GROUPS,)),
-            pltpu.SemaphoreType.DMA((2, GROUPS, LON - 1)),
-            pltpu.SemaphoreType.DMA((2, GROUPS, LON - 1)),
-            pltpu.SemaphoreType.DMA((2, GROUPS, LON - 1)),
-            pltpu.SemaphoreType.DMA((2, GROUPS, LON - 1)),
+            pltpu.SemaphoreType.DMA((2, GROUPS + 1, LON - 1)),
+            pltpu.SemaphoreType.DMA((2, GROUPS + 1, LON - 1)),
+            pltpu.SemaphoreType.DMA((2, GROUPS + 1, LON - 1)),
+            pltpu.SemaphoreType.DMA((2, GROUPS + 1, LON - 1)),
             pltpu.SemaphoreType.DMA((2, 2)),
             pltpu.SemaphoreType.DMA((2, 2)),
         ],
         compiler_params=pltpu.CompilerParams(
             collective_id=0, has_side_effects=True, vmem_limit_bytes=62 * 1024 * 1024
         ),
-    )(quad, norm_gain, ocean_state, zonal_kernel, input_weight, output_weight, table)
+    )(quad, norm_gain, state, zonal_kernel, input_weight, output_weight, table)
+    return jnp.transpose(out, (0, 1, 3, 2))
 
 
 def solution(mesh):

time: 107 us -> 94 us (0.88)
  the two profiles are of different devices: /device:TPU:64 before, /device:TPU:7 now
where the time goes in v1:
time: 94 us; the launch traced here: 93 us
  Pallas kernels  90.4 us (96%)
  local copies, waits for them, and re-layouts  2.61 us (3%)
    pallas_call x1, Pallas kernels, body(): pl.pallas_call(kernel, out_shape=jax.ShapeDtypeStruct((1, ROWS, COLS, C),...  90.4 us
    unnamed x1, local copies, waits for them, and re-layouts  2.61 us

profile of v1, /device:TPU:7, one launch (start us, length us, event | category | flops | bytes accessed | tf_op | source)
XLA Modules:
  0.0 93.0 jit_solution(4022029282993892462)
XLA Ops:
  0.0 90.4 %shard_map.73 = bf16[1,12,96,640]{3,2,1,0:T(8,128)(2,1)} custom-call(f32[196]{0:T(256)} %constant.4.clone.quad_ref, bf16[2,640]{1,0:T(2,128)(2,1)} %gain_ref.1, bf16[1,12,96,640]{3,2,1,0:T(8,128)(2,1)} %bitcast.3, bf16[2,5,256,640]{3,2,1,0:T(8,128)(2,1)} %kern_hbm.1, bf16[2,640,1280]{2,1,0:T(8,128)(2,1)} %w1_hbm.1, bf16[2,1280,640]{2,1,0:T(8,128)(2,1)} %w2_hbm.1, ...), custom_call_target="tpu_custom_call" | custom-call | tf_op jit(solution)/shard_map/pallas_call | solution.py:422
  90.4 2.6 %copy.9 = bf16[1,12,640,96]{2,3,1,0:T(8,128)(2,1)} copy(bf16[1,12,640,96]{2,3,1,0:T(8,128)(2,1)} %bitcast.2) | data formatting | bytes 2949120

commit v2 on v1

--- a/solution.py
+++ b/solution.py
@@ -16,13 +16,13 @@
 BLOCKS = 2
 LON = 8
 ROWS = 12
-SHARE = C // LON
 COLS = W // LON
 HALF = W // 2
 GROUPS = 3
 SPLIT = 32
-A_ORDER = ((0, 1, 2), (1, 2, 0))
-B_ORDER = ((1, 2, 0), (1, 0, 2))
+SHARE = C // LON
+A_PARTS = (((0, 0, SHARE),), ((1, 0, SHARE),), ((2, 0, SPLIT), (3, SPLIT, SHARE - SPLIT)))
+B_PARTS = (((0, 0, SPLIT), (1, SPLIT, SHARE - SPLIT)), ((2, 0, SHARE),), ((3, 0, SHARE),))
 TILES = 9
 MESH = pl.DeviceIdType.MESH
 F32 = jnp.float32
@@ -93,10 +93,10 @@
 
 
 def kernel(
-    quad_ref, gain_ref, x_hbm, kern_hbm, w1_hbm, w2_hbm, f_hbm, out_hbm,
+    quad_ref, gain_ref, x_hbm, kern_hbm, w1_hbm, w2_hbm, f_hbm, out_ref,
     rows_in, xpos, r1, xr, spec, kf, yb, s2, r2, w1t, w2t, hid, nrm, gainb,
     fb, fbt, kraw, w1, w2,
-    in_sem, load_sem, out_sem, a_send, a_recv, b_send, b_recv, h_send, h_recv,
+    in_sem, load_sem, a_send, a_recv, b_send, b_recv, h_send, h_recv,
 ):
     me = lax.axis_index("lon")
     lat = lax.axis_index("lat")
@@ -113,7 +113,7 @@
             x_hbm.at[0, pl.ds(4 * g, 4)], rows_in.at[pl.ds(4 * g, 4)], in_sem.at[g]
         )
 
-    for g in range(GROUPS):
+    for g in (1, 0, 2):
         fetch(g).start()
     loads = [
         pltpu.make_async_copy(src, dst, load_sem.at[i])
@@ -131,16 +131,6 @@
         )
     for other in (up, down):
         pl.semaphore_signal(barrier, inc=1, device_id={"lat": other}, device_id_type=MESH)
-
-    def a_parts(l, g):
-        if g == A_ORDER[l][2]:
-            return [(2, 0, SPLIT), (3, SPLIT, SHARE - SPLIT)]
-        return [(A_ORDER[l].index(g), 0, SHARE)]
-
-    def b_parts(l, g):
-        if g == B_ORDER[l][0]:
-            return [(0, 0, SPLIT), (1, SPLIT, SHARE - SPLIT)]
-        return [(1 + B_ORDER[l].index(g), 0, SHARE)]
 
     def channels(owner, first, count):
         return pl.ds(pl.multiple_of(owner * SHARE + first, 16), count)
@@ -169,19 +159,18 @@
             device_id_type=MESH,
         )
 
-    def halo_copy(l, side):
-        src, dst, other = ((2, 14, up), (12, 0, down))[side]
+    def halo_copy(l, g):
         return pltpu.make_async_remote_copy(
-            src_ref=xr.at[l, pl.ds(src, 2)],
-            dst_ref=xr.at[l, pl.ds(dst, 2)],
-            send_sem=h_send.at[l, side],
-            recv_sem=h_recv.at[l, side],
-            device_id={"lat": other},
+            src_ref=xr.at[l, pl.ds(2 + 5 * g, 2)],
+            dst_ref=xr.at[l, pl.ds(14 - 7 * g, 2)],
+            send_sem=h_send.at[l, g // 2],
+            recv_sem=h_recv.at[l, g // 2],
+            device_id={"lat": lax.rem(lat + lats + g - 1, lats)},
             device_id_type=MESH,
         )
 
-    def start_a(l, g):
-        for part in a_parts(l, g):
+    def start_a(l, g, place):
+        for part in A_PARTS[place]:
             for d in range(1, LON):
                 a_copy(l, g, part, d).start()
         r1[l, me, tiles_of(g)] = xpos[l, tiles_of(g), mine]
@@ -196,12 +185,12 @@
 
         loop(C // 128, piece)
 
-    for g in range(GROUPS):
+    for place, g in enumerate((1, 0, 2)):
         fetch(g).wait()
         pack_input(g)
-        if g == 0:
+        if place == 0:
             pl.semaphore_wait(barrier, LON + 1)
-        start_a(0, g)
+        start_a(0, g, place)
 
     def unit_matrix(n):
         return (
@@ -271,16 +260,13 @@
 
     def transform(l, top, rows, first, count):
         some = pl.ds(first, count)
-
-        def piece(n):
-            at = pl.ds(pl.multiple_of(n * 256, 256), 256)
-            lhs = xr[l, pl.ds(top, rows), some, :].reshape(rows * count, W)
+        lhs = xr[l, pl.ds(top, rows), some, :].reshape(rows * count, W)
+        for n in range(3):
+            at = pl.ds(256 * n, 256)
             part = nn(lhs, fb[:, at])
             for r in range(rows):
                 weight = quad_ref[lat * ROWS + top + r]
                 spec[top + r, some, at] = part[count * r : count * (r + 1)] * weight
-
-        loop(3, piece)
 
     def convolve(l, g, first, count):
         some = pl.ds(first, count)
@@ -308,9 +294,9 @@
 
         loop(count // 16, bands)
 
-        def invert(third):
-            at = pl.multiple_of(256 * third, 256)
-            lhs = yb[:, some, :].reshape(4 * count, W)
+        lhs = yb[:, some, :].reshape(4 * count, W)
+        for third in range(3):
+            at = 256 * third
             part = nn(lhs, fbt[:, pl.ds(at, 256)])
             for half in range(2):
                 tiles = []
@@ -322,8 +308,6 @@
                 for q in range(4):
                     s2[l, 4 * half + q, 3 * g + third, some, :] = packed[q]
 
-        loop(3, invert)
-
     def start_b(l, g, part):
         slot, first, count = part
         for d in range(1, LON):
@@ -343,74 +327,77 @@
 
         loop(3, norm)
 
-        def first(i):
-            at = pl.ds(pl.multiple_of(i * 640, 640), 640)
+        for i in range(FF // 256):
+            at = pl.ds(i * 256, 256)
             hid[at, :] = gelu(nn(w1t[l, at, :], nrm[...])).astype(BF16)
-
-        loop(FF // 640, first)
         out = nn(w2t[l], hid[...])
         for t in range(3):
             old = r2[l, 3 * g + t].astype(F32)
             new = (old + out[:, 128 * t : 128 * (t + 1)]).astype(BF16)
-            if l == 0:
-                xpos[1, 3 * g + t] = new
-            else:
-                lons = pl.ds(32 * t, 32)
-                for i in range(C // 128):
-                    turned = new[128 * i : 128 * (i + 1), :].T
-                    for r in range(4):
-                        rows_in[4 * g + r, lons, pl.ds(128 * i, 128)] = turned[
-                            32 * r : 32 * (r + 1), :
-                        ]
-
-    def store(g):
-        return pltpu.make_async_copy(
-            rows_in.at[pl.ds(4 * g, 4)], out_hbm.at[0, pl.ds(4 * g, 4)], out_sem.at[g]
-        )
+            xpos[1 - l, 3 * g + t] = new
+
+    def finish(g):
+        def piece(i):
+            at = pl.ds(pl.multiple_of(i * 128, 128), 128)
+            for third in range(3):
+                turned = xpos[0, 3 * g + third, at, :].T
+                for r in range(4):
+                    out_ref[0, 4 * g + r, pl.ds(32 * third, 32), at] = turned[
+                        32 * r : 32 * (r + 1), :
+                    ]
+
+        loop(C // 128, piece)
 
     def take(l, g, part):
         for d in range(1, LON):
             a_copy(l, g, part, d).wait_recv()
         unpack(l, g, *part[1:])
-        if part[1] + part[2] == SHARE and g != 1:
-            halo_copy(l, g // 2).start()
         transform(l, 2 + 4 * g, 4, *part[1:])
 
     def give(l, g, part):
         convolve(l, g, *part[1:])
         start_b(l, g, part)
 
-    for l in range(BLOCKS):
-        for g in A_ORDER[l][:2]:
-            take(l, g, a_parts(l, g)[0])
-        last = A_ORDER[l][2]
-        for arrived, ready in zip(a_parts(l, last), b_parts(l, 1)):
-            take(l, last, arrived)
+    def block(l):
+        early, late = 2 * l, 2 - 2 * l
+        take(l, 1, A_PARTS[0][0])
+        take(l, early, A_PARTS[1][0])
+        halo_copy(l, early).start()
+        for place, (arrived, ready) in enumerate(zip(A_PARTS[2], B_PARTS[0])):
+            take(l, late, arrived)
+            if place == 1:
+                halo_copy(l, late).start()
             give(l, 1, ready)
-        for g in B_ORDER[l][1:]:
-            halo_copy(l, 1 - g // 2).wait_recv()
-            transform(l, 0 if g == 0 else ROWS + 2, 2, 0, SHARE)
-            give(l, g, b_parts(l, g)[0])
-        for g in B_ORDER[l]:
-            for part in b_parts(l, g):
+        for place, g in ((1, late), (2, early)):
+            halo_copy(l, 2 - g).wait_recv()
+            transform(l, 7 * g, 2, 0, SHARE)
+            give(l, g, B_PARTS[place][0])
+        for place, g in enumerate((1, late, early)):
+            for part in B_PARTS[place]:
                 for d in range(1, LON):
                     b_copy(l, g, part, d).wait_recv()
             feed_forward(l, g)
-            if l == 0:
-                start_a(1, g)
-            else:
-                store(g).start()
-    for l in range(BLOCKS):
-        for g in range(GROUPS):
+
+            @pl.when(l == 0)
+            def _():
+                start_a(1, g, place)
+
+            @pl.when(l == BLOCKS - 1)
+            def _():
+                finish(g)
+
+        for a_place, g in enumerate((1, early, late)):
             for d in range(1, LON):
-                for part in a_parts(l, g):
+                for part in A_PARTS[a_place]:
                     a_copy(l, g, part, d).wait_send()
-                for part in b_parts(l, g):
+        for b_place, g in enumerate((1, late, early)):
+            for d in range(1, LON):
+                for part in B_PARTS[b_place]:
                     b_copy(l, g, part, d).wait_send()
-        for side in range(2):
-            halo_copy(l, side).wait_send()
-    for g in range(GROUPS):
-        store(g).wait()
+        halo_copy(l, early).wait_send()
+        halo_copy(l, late).wait_send()
+
+    loop(BLOCKS, block)
 
 
 def body(ocean_state, zonal_kernel, norm_gain, input_weight, output_weight):
@@ -421,13 +408,13 @@
     hbm = pl.BlockSpec(memory_space=pl.ANY)
     out = pl.pallas_call(
         kernel,
-        out_shape=jax.ShapeDtypeStruct((1, ROWS, COLS, C), BF16),
+        out_shape=pltpu.VMEM((1, ROWS, COLS, C), BF16),
         in_specs=[
             pl.BlockSpec(memory_space=pltpu.SMEM),
             pl.BlockSpec(memory_space=pltpu.VMEM),
             hbm, hbm, hbm, hbm, hbm,
         ],
-        out_specs=hbm,
+        out_specs=pl.BlockSpec(memory_space=pltpu.VMEM),
         scratch_shapes=[
             pltpu.VMEM((ROWS, COLS, C), BF16),
             pltpu.VMEM((2, TILES, C, 128), BF16),
@@ -450,7 +437,6 @@
             pltpu.VMEM((BLOCKS, FF, C), BF16),
             pltpu.SemaphoreType.DMA((GROUPS,)),
             pltpu.SemaphoreType.DMA((4,)),
-            pltpu.SemaphoreType.DMA((GROUPS,)),
             pltpu.SemaphoreType.DMA((2, GROUPS + 1, LON - 1)),
             pltpu.SemaphoreType.DMA((2, GROUPS + 1, LON - 1)),
             pltpu.SemaphoreType.DMA((2, GROUPS + 1, LON - 1)),
@@ -459,7 +445,7 @@
             pltpu.SemaphoreType.DMA((2, 2)),
         ],
         compiler_params=pltpu.CompilerParams(
-            collective_id=0, has_side_effects=True, vmem_limit_bytes=62 * 1024 * 1024
+            collective_id=0, has_side_effects=True, vmem_limit_bytes=54 * 1024 * 1024
         ),
     )(quad, norm_gain, state, zonal_kernel, input_weight, output_weight, table)
     return jnp.transpose(out, (0, 1, 3, 2))

time: 94 us -> 88 us (0.936)
  Pallas kernels: 90.4 us -> 86.7 us
  local copies, waits for them, and re-layouts: 2.61 us -> 1.11 us
    pallas_call x1, Pallas kernels: 90.4 us -> 86.7 us  [body(): pl.pallas_call(kernel, out_shape=pltpu.VMEM((1, ROWS, COLS, C), BF16), in...]
    unnamed x1, local copies, waits for them, and re-layouts: 2.61 us -> 1.11 us
where the time goes in v2:
time: 88 us; the launch traced here: 87.8 us
  Pallas kernels  86.7 us (99%)
  local copies, waits for them, and re-layouts  1.11 us (1%)
    pallas_call x1, Pallas kernels, body(): pl.pallas_call(kernel, out_shape=pltpu.VMEM((1, ROWS, COLS, C), BF16), in...  86.7 us

profile of v2, /device:TPU:7, one launch (start us, length us, event | category | flops | bytes accessed | tf_op | source)
XLA Modules:
  0.0 87.8 jit_solution(11729322188172713783)
XLA Ops:
  0.0 86.7 %shard_map.73 = bf16[1,12,96,640]{3,2,1,0:T(8,128)(2,1)S(1)} custom-call(f32[196]{0:T(256)} %constant.4.clone.quad_ref, bf16[2,640]{1,0:T(2,128)(2,1)} %gain_ref.1, bf16[1,12,96,640]{3,2,1,0:T(8,128)(2,1)} %bitcast.3, bf16[2,5,256,640]{3,2,1,0:T(8,128)(2,1)} %kern_hbm.1, bf16[2,640,1280]{2,1,0:T(8,128)(2,1)} %w1_hbm.1, bf16[2,1280,640]{2,1,0:T(8,128)(2,1)} %w2_hbm.1, ...), custom_call_target="tpu_custom_call" | custom-call | tf_op jit(solution)/shard_map/pallas_call | solution.py:409
  86.7 1.1 %copy.9 = bf16[1,12,640,96]{2,3,1,0:T(8,128)(2,1)} copy(bf16[1,12,640,96]{2,3,1,0:T(8,128)(2,1)S(1)} %bitcast.2) | data formatting | bytes 2949120

commit v3 on v2

--- a/solution.py
+++ b/solution.py
@@ -19,7 +19,7 @@
 COLS = W // LON
 HALF = W // 2
 GROUPS = 3
-SPLIT = 32
+SPLIT = 48
 SHARE = C // LON
 A_PARTS = (((0, 0, SHARE),), ((1, 0, SHARE),), ((2, 0, SPLIT), (3, SPLIT, SHARE - SPLIT)))
 B_PARTS = (((0, 0, SPLIT), (1, SPLIT, SHARE - SPLIT)), ((2, 0, SHARE),), ((3, 0, SHARE),))
@@ -348,11 +348,17 @@
 
         loop(C // 128, piece)
 
-    def take(l, g, part):
+    def take(l, g, part, rim=False):
         for d in range(1, LON):
             a_copy(l, g, part, d).wait_recv()
         unpack(l, g, *part[1:])
+        if rim:
+            halo_copy(l, g).start()
         transform(l, 2 + 4 * g, 4, *part[1:])
+
+    def take_rim(l, g):
+        halo_copy(l, 2 - g).wait_recv()
+        transform(l, 7 * g, 2, 0, SHARE)
 
     def give(l, g, part):
         convolve(l, g, *part[1:])
@@ -361,17 +367,15 @@
     def block(l):
         early, late = 2 * l, 2 - 2 * l
         take(l, 1, A_PARTS[0][0])
-        take(l, early, A_PARTS[1][0])
-        halo_copy(l, early).start()
-        for place, (arrived, ready) in enumerate(zip(A_PARTS[2], B_PARTS[0])):
-            take(l, late, arrived)
-            if place == 1:
-                halo_copy(l, late).start()
-            give(l, 1, ready)
-        for place, g in ((1, late), (2, early)):
-            halo_copy(l, 2 - g).wait_recv()
-            transform(l, 7 * g, 2, 0, SHARE)
-            give(l, g, B_PARTS[place][0])
+        take(l, early, A_PARTS[1][0], rim=True)
+        take(l, late, A_PARTS[2][0])
+        give(l, 1, B_PARTS[0][0])
+        take_rim(l, late)
+        take(l, late, A_PARTS[2][1], rim=True)
+        give(l, 1, B_PARTS[0][1])
+        give(l, late, B_PARTS[1][0])
+        take_rim(l, early)
+        give(l, early, B_PARTS[2][0])
         for place, g in enumerate((1, late, early)):
             for part in B_PARTS[place]:
                 for d in range(1, LON):

time: 88 us -> 91 us (1.034)
  Pallas kernels: 86.7 us -> 89.7 us
    pallas_call x1, Pallas kernels: 86.7 us -> 89.7 us  [body(): pl.pallas_call(kernel, out_shape=pltpu.VMEM((1, ROWS, COLS, C), BF16), in...]
where the time goes in v3:
time: 91 us; the launch traced here: 90.9 us
  Pallas kernels  89.7 us (99%)
  local copies, waits for them, and re-layouts  1.11 us (1%)
    pallas_call x1, Pallas kernels, body(): pl.pallas_call(kernel, out_shape=pltpu.VMEM((1, ROWS, COLS, C), BF16), in...  89.7 us

profile of v3, /device:TPU:7, one launch (start us, length us, event | category | flops | bytes accessed | tf_op | source)
XLA Modules:
  0.0 90.9 jit_solution(12802123481210063439)
XLA Ops:
  0.0 89.7 %shard_map.73 = bf16[1,12,96,640]{3,2,1,0:T(8,128)(2,1)S(1)} custom-call(f32[196]{0:T(256)} %constant.4.clone.quad_ref, bf16[2,640]{1,0:T(2,128)(2,1)} %gain_ref.1, bf16[1,12,96,640]{3,2,1,0:T(8,128)(2,1)} %bitcast.3, bf16[2,5,256,640]{3,2,1,0:T(8,128)(2,1)} %kern_hbm.1, bf16[2,640,1280]{2,1,0:T(8,128)(2,1)} %w1_hbm.1, bf16[2,1280,640]{2,1,0:T(8,128)(2,1)} %w2_hbm.1, ...), custom_call_target="tpu_custom_call" | custom-call | tf_op jit(solution)/shard_map/pallas_call | solution.py:413
  89.7 1.1 %copy.9 = bf16[1,12,640,96]{2,3,1,0:T(8,128)(2,1)} copy(bf16[1,12,640,96]{2,3,1,0:T(8,128)(2,1)S(1)} %bitcast.2) | data formatting | bytes 2949120

commit v4 on v2

--- a/solution.py
+++ b/solution.py
@@ -348,10 +348,12 @@
 
         loop(C // 128, piece)
 
-    def take(l, g, part):
+    def take(l, g, part, rim=False):
         for d in range(1, LON):
             a_copy(l, g, part, d).wait_recv()
         unpack(l, g, *part[1:])
+        if rim:
+            halo_copy(l, g).start()
         transform(l, 2 + 4 * g, 4, *part[1:])
 
     def give(l, g, part):
@@ -361,12 +363,9 @@
     def block(l):
         early, late = 2 * l, 2 - 2 * l
         take(l, 1, A_PARTS[0][0])
-        take(l, early, A_PARTS[1][0])
-        halo_copy(l, early).start()
+        take(l, early, A_PARTS[1][0], rim=True)
         for place, (arrived, ready) in enumerate(zip(A_PARTS[2], B_PARTS[0])):
-            take(l, late, arrived)
-            if place == 1:
-                halo_copy(l, late).start()
+            take(l, late, arrived, rim=place == 1)
             give(l, 1, ready)
         for place, g in ((1, late), (2, early)):
             halo_copy(l, 2 - g).wait_recv()

time: 88 us -> 90.1 us (1.024)
  Pallas kernels: 86.7 us -> 88.9 us
    pallas_call x1, Pallas kernels: 86.7 us -> 88.9 us  [body(): pl.pallas_call(kernel, out_shape=pltpu.VMEM((1, ROWS, COLS, C), BF16), in...]
where the time goes in v4:
time: 90.1 us; the launch traced here: 90 us
  Pallas kernels  88.9 us (99%)
  local copies, waits for them, and re-layouts  1.11 us (1%)
    pallas_call x1, Pallas kernels, body(): pl.pallas_call(kernel, out_shape=pltpu.VMEM((1, ROWS, COLS, C), BF16), in...  88.9 us

profile of v4, /device:TPU:7, one launch (start us, length us, event | category | flops | bytes accessed | tf_op | source)
XLA Modules:
  0.0 90.0 jit_solution(1207414821919293439)
XLA Ops:
  0.0 88.9 %shard_map.73 = bf16[1,12,96,640]{3,2,1,0:T(8,128)(2,1)S(1)} custom-call(f32[196]{0:T(256)} %constant.4.clone.quad_ref, bf16[2,640]{1,0:T(2,128)(2,1)} %gain_ref.1, bf16[1,12,96,640]{3,2,1,0:T(8,128)(2,1)} %bitcast.3, bf16[2,5,256,640]{3,2,1,0:T(8,128)(2,1)} %kern_hbm.1, bf16[2,640,1280]{2,1,0:T(8,128)(2,1)} %w1_hbm.1, bf16[2,1280,640]{2,1,0:T(8,128)(2,1)} %w2_hbm.1, ...), custom_call_target="tpu_custom_call" | custom-call | tf_op jit(solution)/shard_map/pallas_call | solution.py:408
  88.9 1.1 %copy.9 = bf16[1,12,640,96]{2,3,1,0:T(8,128)(2,1)} copy(bf16[1,12,640,96]{2,3,1,0:T(8,128)(2,1)S(1)} %bitcast.2) | data formatting | bytes 2949120
